TPU v7x, 32 devices: a whole 2x2x4 slice. The times are simulated.
32 devices in a mesh: cp: 8 (over z, x), tp: 4 (over y, core).
Axes of the slice: x: 2, y: 2, z: 4, core: 2. Of those that a mesh axis runs over, the one named last changes fastest.
Arguments:
- queries: bfloat16 [1536, 2048], P('cp', 'tp'), may hold values from -128 to 128
- keys: bfloat16 [1536, 256], P('cp'), may hold values from -6 to 6
- values: bfloat16 [1536, 256], P('cp'), may hold values from -6 to 6
- positions: int32 [1536], replicated, may hold values from 0 to 1535, as said below
- out_weight: bfloat16 [2048, 8192], P('tp'), may hold values from -0.125 to 0.125
Outputs:
- mixed: bfloat16 [1536, 8192], P(('cp', 'tp'))
Inputs may be any that keep to these rules, and one draw needn't show every extreme that they name: positions is a permutation of 0 to 1535. The tokens stored at indices d * 192 to (d + 1) * 192 - 1 form two runs of 96 consecutive positions, the first starting at b * 96 and the second at (15 - b) * 96 for some b, each b used by one d.
All inputs are finite; a program needn't handle non-finite values.
Results may differ from a plain program's by a relative error of at most 0.013.
Values may be sent and summed in bfloat16 or wider, within the bound.
A program may use at most 128 MiB of HBM per device.

v0:
```python
import jax
import jax.numpy as jnp
from jax import lax
from jax.sharding import PartitionSpec as P

HEAD = 128
GROUP = 8


def shards(queries, keys, values, positions, out_weight):
    tok_rows = queries.shape[0]
    head_count = queries.shape[1] // HEAD
    score_scale = HEAD ** (-0.5)
    kv_group = lax.axis_index("tp") * head_count // GROUP
    own_keys = lax.dynamic_slice_in_dim(keys, kv_group * HEAD, HEAD, 1)
    own_values = lax.dynamic_slice_in_dim(values, kv_group * HEAD, HEAD, 1)
    query_pos = lax.dynamic_slice_in_dim(positions, lax.axis_index("cp") * tok_rows, tok_rows, 0)
    local_queries = queries.reshape(tok_rows, head_count, HEAD)
    run_max = jnp.full((tok_rows, head_count), -1e30, jnp.float32)
    arrived_keys = lax.all_gather(own_keys, "cp", axis=0, tiled=True)
    arrived_values = lax.all_gather(own_values, "cp", axis=0, tiled=True)
    allowed = (positions[None, :] <= query_pos[:, None])[:, None, :]
    scores = (
        jnp.einsum("qhd,kd->qhk", local_queries, arrived_keys, preferred_element_type=jnp.float32)
        * score_scale
    )
    scores = jnp.where(allowed, scores, -1e30)
    new_max = jnp.maximum(run_max, jnp.max(scores, axis=-1))
    weights = jnp.where(allowed, jnp.exp(scores - new_max[:, :, None]), 0.0)
    run_sum = jnp.sum(weights, axis=-1)
    run_out = jnp.einsum(
        "qhk,kd->qhd",
        weights.astype(jnp.bfloat16),
        arrived_values,
        preferred_element_type=jnp.float32,
    )
    final_state = (new_max, run_sum, run_out)
    run_max, run_sum, run_out = final_state
    attended = (
        (run_out / run_sum[:, :, None]).astype(jnp.bfloat16).reshape(tok_rows, head_count * HEAD)
    )
    return lax.psum_scatter(
        jnp.dot(attended, out_weight, preferred_element_type=jnp.float32).astype(jnp.bfloat16),
        "tp",
        scatter_dimension=0,
        tiled=True,
    )


def solution(mesh):
    in_specs = (P("cp", "tp"), P("cp", None), P("cp", None), P(), P("tp", None))
    out_specs = P(("cp", "tp"), None)
    return jax.shard_map(shards, mesh=mesh, in_specs=in_specs, out_specs=out_specs, check_vma=False)
```

profile of v0, /device:TPU:0, one launch (start us, length us, event | category | flops | bytes accessed | tf_op | source)
XLA Modules:
  0.0 127.3 jit_solution(13655687156293303523)
XLA Ops:
  6.5 0.0 copy-start
  6.5 0.0 copy-start.1
  6.5 0.0 reduce-scatter.2.cloned.1.call-start
  6.5 0.8 constant_dynamic-slice_fusion.1
  7.4 32.8 %all_gather.6 = bf16[1536,128]{1,0:T(8,128)(2,1)S(1)} all-gather(bf16[192,128]{1,0:T(8,128)(2,1)S(1)} %constant_dynamic-slice_fusion.1), channel_id=1, replica_groups=mesh['cp'=8,'tp'=4] {'cp'}, dimensions={0}, use_global_device_ids=true | all-gather | bytes 442368 | tf_op jit(solution)/shard_map/all_gather | solution.py:20
  40.2 0.8 dynamic_slice.9
  40.9 0.9 broadcast_compare_fusion
  41.9 0.0 copy-done
  41.9 1.1 fusion
  43.0 0.0 copy-done.1
  43.0 31.0 %all_gather.7 = bf16[1536,128]{1,0:T(8,128)(2,1)S(1)} all-gather(bf16[192,128]{1,0:T(8,128)(2,1)S(1)} %constant_dynamic-slice_fusion), channel_id=1, replica_groups=mesh['cp'=8,'tp'=4] {'cp'}, dimensions={0}, use_global_device_ids=true | all-gather | bytes 442368 | tf_op jit(solution)/shard_map/all_gather | solution.py:21
  74.0 0.0 slice-start
  74.0 1.5 %fusion.1 = f32[192,4]{0,1:T(4,128)S(1)} fusion(f32[1536,192,4]{0,1,2:T(8,128)S(1)} %get-tuple-element.6, f32[192,4]{0,1:T(4,128)S(1)} %broadcast_maximum_fusion, pred[192,1536]{1,0:T(8,128)(4,1)S(1)} %broadcast_compare_fusion), kind=kLoop, calls=%fused_computation.4 | loop fusion | flops 5897472 | bytes 5019648 | tf_op jit(solution)/shard_map/reduce_sum | solution.py:30
  75.5 0.0 slice-start.1
  75.5 1.4 %fusion.12 = bf16[4,24,8,128]{3,2,1,0:T(8,128)(2,1)S(1)} fusion(f32[1536,192,4]{0,1,2:T(8,128)S(1)} %get-tuple-element.6, f32[192,4]{0,1:T(4,128)S(1)} %broadcast_maximum_fusion, pred[192,1536]{1,0:T(8,128)(4,1)S(1)} %broadcast_compare_fusion, bf16[1536,128]{1,0:T(8,128)(2,1)S(1)} %all_gather.7, f32[192,4]{0,1:T(4,128)S(1)} %fusion.1), kind=kOutput, calls=%fused_computation.10 | convolution fusion | flops 308084736 | bytes 5609472 | tf_op jit(solution)/shard_map/qhk,kd->qhd/dot_general | solution.py:31
  76.9 0.0 slice-done
  76.9 0.9 slice-done.1
  77.8 3.5 %convolution_convert_fusion = bf16[192,8192]{1,0:T(8,128)(2,1)} fusion(bf16[512,8192]{1,0:T(8,128)(2,1)S(1)} %bitcast.41, bf16[4,24,8,128]{3,2,1,0:T(8,128)(2,1)S(1)} %fusion.12), kind=kOutput, calls=%fused_computation | convolution fusion | flops 1612185600 | bytes 11730944 | tf_op jit(solution)/shard_map/dot_general | solution.py:43
  81.3 0.0 reduce-scatter.2.cloned.1.call-update
  81.3 39.2 %reduce-scatter.2.cloned.1.call-done = bf16[48,8192]{1,0:T(8,128)(2,1)} async-done(((bf16[192,8192]{1,0:T(8,128)(2,1)}), bf16[48,8192]{1,0:T(8,128)(2,1)}) %reduce-scatter.2.cloned.1.call-update) | async-done | bytes 786448 | tf_op jit(solution)/shard_map/reduce_scatter | solution.py:42
  (3 shorter events, 0.0 us)
Async XLA Ops:
  6.5 35.3 %copy-start = (bf16[192,512]{1,0:T(8,128)(2,1)S(1)}, bf16[192,512]{1,0:T(8,128)(2,1)}, u32[]{:S(2)}) copy-start(bf16[192,512]{1,0:T(8,128)(2,1)} %param.5) | copy-start | bytes 589828
  6.5 36.4 %copy-start.1 = (bf16[192,256]{1,0:T(8,128)(2,1)S(1)}, bf16[192,256]{1,0:T(8,128)(2,1)}, u32[]{:S(2)}) copy-start(bf16[192,256]{1,0:T(8,128)(2,1)} %param.7) | copy-start | bytes 294916
  6.5 114.0 %reduce-scatter.2.cloned.1.call-start = ((), (), s32[]{:S(2)}) async-start(), calls=%async_computation.1 | async-start | bytes 3932160 | tf_op jit(solution)/shard_map/reduce_scatter | solution.py:42
  74.0 2.9 %slice-start = ((s8[8388608]{0:T(1024)(128)(4,1)}), s8[4194304]{0:T(1024)(128)(4,1)S(1)}, s32[]{:S(2)}) async-start(s8[8388608]{0:T(1024)(128)(4,1)} %bitcast.40), calls=%async_computation.2 | async-start | bytes 8388608
  75.5 2.4 %slice-start.1 = ((s8[8388608]{0:T(1024)(128)(4,1)}), s8[4194304]{0:T(1024)(128)(4,1)S(1)}, s32[]{:S(2)}) async-start(s8[8388608]{0:T(1024)(128)(4,1)} %bitcast.40), calls=%async_computation.3 | async-start | bytes 8388608
Sparse Core Ops, SparseCore 0:
  81.4 39.0 reduce-scatter.1
where the time goes:
time: 128 us; the launch traced here: 127 us
  blocking collectives  63.7 us (50%)
  waiting for transfers between devices  39.2 us (31%)
  between operations  13.4 us (10%)
  matrix products  5.98 us (5%)
  local copies, waits for them, and re-layouts  2.58 us (2%)
  other arithmetic  2.41 us (2%)
    reduce_scatter x1, waiting for transfers between devices, shards(): lax.psum_scatter(jnp.dot(attended, out_weight, preferred_element_type=jnp...  39.2 us
    all_gather x1, blocking collectives, shards(): arrived_keys = lax.all_gather(own_keys, 'cp', axis=0, tiled=True)  32.8 us
    all_gather x1, blocking collectives, shards(): arrived_values = lax.all_gather(own_values, 'cp', axis=0, tiled=True)  31 us
    dot_general x1, matrix products, shards(): jnp.dot(attended, out_weight, preferred_element_type=jnp.float32)  3.47 us
  transfers between devices with their start and end apart: 1, of which 1 were waited for; matrix products, arithmetic and copies ran while one was open for 0% of the time, Pallas kernels for 0%

commit v1 on v0

--- a/solution.py
+++ b/solution.py
@@ -1,3 +1,4 @@
+import functools
 import jax
 import jax.numpy as jnp
 from jax import lax
@@ -5,6 +6,16 @@
 
 HEAD = 128
 GROUP = 8
+
+
+def remake_strings(x_part, axis_key, d0):
+    a_now = lax.axis_size(axis_key)
+    latest = jnp.stack([x_part] * a_now, 0)
+    after = lax.all_to_all(latest, axis_name=axis_key, split_axis=0, concat_axis=0)
+    return jnp.concatenate(after, d0)
+
+
+_fit_lines = functools.partial(remake_strings, axis_key="cp", d0=0)
 
 
 def shards(queries, keys, values, positions, out_weight):
@@ -17,7 +28,7 @@
     query_pos = lax.dynamic_slice_in_dim(positions, lax.axis_index("cp") * tok_rows, tok_rows, 0)
     local_queries = queries.reshape(tok_rows, head_count, HEAD)
     run_max = jnp.full((tok_rows, head_count), -1e30, jnp.float32)
-    arrived_keys = lax.all_gather(own_keys, "cp", axis=0, tiled=True)
+    arrived_keys = _fit_lines(own_keys)
     arrived_values = lax.all_gather(own_values, "cp", axis=0, tiled=True)
     allowed = (positions[None, :] <= query_pos[:, None])[:, None, :]
     scores = (

time: 128 us -> 104 us (0.81)
  blocking collectives: 63.7 us -> 34.2 us
  starting transfers between devices: 0.01 us -> 7.32 us
  waiting for transfers between devices: 39.2 us -> 36.4 us
  local copies, waits for them, and re-layouts: 2.58 us -> 4.16 us
    all_gather x1 -> x0, blocking collectives: 32.8 us -> none  [shards(): arrived_keys = lax.all_gather(own_keys, 'cp', axis=0, tiled=True)]
    all_to_all x0 -> x1, starting transfers between devices: none -> 7.28 us  [remake_strings(): lax.all_to_all(latest, axis_name=axis_key, split_axis=0, concat_axis=0)]
    all_gather x1, blocking collectives: 31 us -> 34.2 us  [shards(): arrived_values = lax.all_gather(own_values, 'cp', axis=0, tiled=True)]
    reduce_scatter x1, waiting for transfers between devices: 39.2 us -> 36.3 us  [shards(): lax.psum_scatter(jnp.dot(attended, out_weight, preferred_element_type=jnp...]
  transfers between devices with their start and end apart: 1 -> 2, of which waited for: 1 -> 1; matrix products, arithmetic and copies ran while one was open for 0% -> 2% of each run, Pallas kernels for 0% -> 0%
where the time goes in v1:
time: 104 us
  waiting for transfers between devices  36.4 us (35%)
  blocking collectives  34.2 us (33%)
  between operations  13.5 us (13%)
  starting transfers between devices  7.32 us (7%)
  matrix products  5.98 us (6%)
  local copies, waits for them, and re-layouts  4.16 us (4%)
  other arithmetic  2.41 us (2%)
    reduce_scatter x1, waiting for transfers between devices, shards(): lax.psum_scatter(jnp.dot(attended, out_weight, preferred_element_type=jnp...  36.3 us
    all_gather x1, blocking collectives, shards(): arrived_values = lax.all_gather(own_values, 'cp', axis=0, tiled=True)  34.2 us
    all_to_all x1, starting transfers between devices, remake_strings(): lax.all_to_all(latest, axis_name=axis_key, split_axis=0, concat_axis=0)  7.28 us
    dot_general x1, matrix products, shards(): jnp.dot(attended, out_weight, preferred_element_type=jnp.float32)  3.46 us
  transfers between devices with their start and end apart: 2, of which 1 were waited for; matrix products, arithmetic and copies ran while one was open for 2% of the time, Pallas kernels for 0%

profile of v1, /device:TPU:0, one launch (start us, length us, event | category | flops | bytes accessed | tf_op | source)
XLA Modules:
  0.0 103.9 jit_solution(4264123524561305348)
XLA Ops:
  6.5 0.0 copy-start
  6.5 0.8 constant_dynamic-slice_fusion.1
  7.4 0.8 stack.2
  8.2 7.3 %all-to-all-start = ((bf16[8,192,128]{2,1,0:T(8,128)(2,1)}), bf16[8,192,128]{2,1,0:T(8,128)(2,1)S(1)}, u32[]{:S(2)}, u32[]{:S(2)}) async-start(bf16[8,192,128]{2,1,0:T(8,128)(2,1)} %stack.2), calls=%async_computation | async-start | bytes 786432 | tf_op jit(solution)/shard_map/all_to_all | solution.py:14
  15.5 0.0 reduce-scatter.2.cloned.1.call-start
  15.5 0.8 dynamic_slice.9
  16.3 0.8 constant_dynamic-slice_fusion
  17.1 34.2 %all_gather.3 = bf16[1536,128]{1,0:T(8,128)(2,1)S(1)} all-gather(bf16[192,128]{1,0:T(8,128)(2,1)S(1)} %constant_dynamic-slice_fusion), channel_id=1, replica_groups=mesh['cp'=8,'tp'=4] {'cp'}, dimensions={0}, use_global_device_ids=true | all-gather | bytes 442368 | tf_op jit(solution)/shard_map/all_gather | solution.py:32
  51.3 0.9 broadcast_compare_fusion
  52.2 0.0 all-to-all-done
  52.2 0.0 copy-done
  52.3 1.1 %fusion = (f32[192,4]{0,1:T(4,128)S(1)}, f32[1536,192,4]{0,1,2:T(8,128)S(1)}) fusion(pred[192,1536]{1,0:T(8,128)(4,1)S(1)} %broadcast_compare_fusion, bf16[1536,128,1]{1,0,2:T(8,128)(2,1)S(1)} %bitcast.41, bf16[192,512]{1,0:T(8,128)(2,1)S(1)} %copy-done), kind=kOutput, calls=%fused_computation.3 | convolution fusion | flops 305528064 | bytes 5606400 | tf_op jit(solution)/shard_map/qhd,kd->qhk/dot_general | solution.py:35
  53.4 0.0 slice-start
  53.4 1.5 %fusion.1 = f32[192,4]{0,1:T(4,128)S(1)} fusion(f32[1536,192,4]{0,1,2:T(8,128)S(1)} %get-tuple-element.6, f32[192,4]{0,1:T(4,128)S(1)} %broadcast_maximum_fusion, pred[192,1536]{1,0:T(8,128)(4,1)S(1)} %broadcast_compare_fusion), kind=kLoop, calls=%fused_computation.4 | loop fusion | flops 5897472 | bytes 5019648 | tf_op jit(solution)/shard_map/reduce_sum | solution.py:41
  54.9 0.0 slice-start.1
  54.9 1.4 %fusion.12 = bf16[4,24,8,128]{3,2,1,0:T(8,128)(2,1)S(1)} fusion(f32[1536,192,4]{0,1,2:T(8,128)S(1)} %get-tuple-element.6, f32[192,4]{0,1:T(4,128)S(1)} %broadcast_maximum_fusion, pred[192,1536]{1,0:T(8,128)(4,1)S(1)} %broadcast_compare_fusion, bf16[1536,128]{1,0:T(8,128)(2,1)S(1)} %all_gather.3, f32[192,4]{0,1:T(4,128)S(1)} %fusion.1), kind=kOutput, calls=%fused_computation.10 | convolution fusion | flops 308084736 | bytes 5609472 | tf_op jit(solution)/shard_map/qhk,kd->qhd/dot_general | solution.py:42
  56.3 0.0 slice-done
  56.3 0.9 slice-done.1
  57.2 3.5 %convolution_convert_fusion = bf16[192,8192]{1,0:T(8,128)(2,1)} fusion(bf16[512,8192]{1,0:T(8,128)(2,1)S(1)} %bitcast.40, bf16[4,24,8,128]{3,2,1,0:T(8,128)(2,1)S(1)} %fusion.12), kind=kOutput, calls=%fused_computation | convolution fusion | flops 1612185600 | bytes 11730944 | tf_op jit(solution)/shard_map/dot_general | solution.py:54
  60.7 0.0 reduce-scatter.2.cloned.1.call-update
  60.7 36.3 %reduce-scatter.2.cloned.1.call-done = bf16[48,8192]{1,0:T(8,128)(2,1)} async-done(((bf16[192,8192]{1,0:T(8,128)(2,1)}), bf16[48,8192]{1,0:T(8,128)(2,1)}) %reduce-scatter.2.cloned.1.call-update) | async-done | bytes 786448 | tf_op jit(solution)/shard_map/reduce_scatter | solution.py:53
  (2 shorter events, 0.0 us)
Async XLA Ops:
  6.5 45.7 %copy-start = (bf16[192,512]{1,0:T(8,128)(2,1)S(1)}, bf16[192,512]{1,0:T(8,128)(2,1)}, u32[]{:S(2)}) copy-start(bf16[192,512]{1,0:T(8,128)(2,1)} %param.5) | copy-start | bytes 589828
  8.2 44.1 %all-to-all-start = ((bf16[8,192,128]{2,1,0:T(8,128)(2,1)}), bf16[8,192,128]{2,1,0:T(8,128)(2,1)S(1)}, u32[]{:S(2)}, u32[]{:S(2)}) async-start(bf16[8,192,128]{2,1,0:T(8,128)(2,1)} %stack.2), calls=%async_computation | async-start | bytes 786432 | tf_op jit(solution)/shard_map/all_to_all | solution.py:14
  15.5 81.6 %reduce-scatter.2.cloned.1.call-start = ((), (), s32[]{:S(2)}) async-start(), calls=%async_computation.2 | async-start | bytes 3932160 | tf_op jit(solution)/shard_map/reduce_scatter | solution.py:53
  53.4 2.9 %slice-start = ((s8[8388608]{0:T(1024)(128)(4,1)}), s8[4194304]{0:T(1024)(128)(4,1)S(1)}, s32[]{:S(2)}) async-start(s8[8388608]{0:T(1024)(128)(4,1)} %bitcast.39), calls=%async_computation.3 | async-start | bytes 8388608
  54.9 2.4 %slice-start.1 = ((s8[8388608]{0:T(1024)(128)(4,1)}), s8[4194304]{0:T(1024)(128)(4,1)S(1)}, s32[]{:S(2)}) async-start(s8[8388608]{0:T(1024)(128)(4,1)} %bitcast.39), calls=%async_computation.4 | async-start | bytes 8388608
Sparse Core Ops, SparseCore 0:
  60.8 36.1 reduce-scatter.1
